TPU v7x, 32 devices: a whole 2x2x4 slice. The times are simulated.
32 devices in a mesh: replica: 8 (over y, x, core), tensor: 4 (over z).
Axes of the slice: x: 2, y: 2, z: 4, core: 2. Of those that a mesh axis runs over, the one named last changes fastest.
Arguments:
- weights: bfloat16 [8, 7168, 2048], P('replica', 'tensor'), may hold values from -6 to 6
- hidden: bfloat16 [8, 2, 512, 7168], P('replica', None, None, 'tensor'), may hold values from -6 to 6
- targets: bfloat16 [8, 2, 512, 2048], P('replica'), may hold values from -6 to 6
- norm_gain: float32 [2048], replicated, may hold values from 0.5 to 2
- stragglers: int32 [2, 8], replicated, may hold values 0 or 1
Outputs:
- new_weights: bfloat16 [8, 7168, 2048], P('replica', 'tensor')
All inputs are finite; a program needn't handle non-finite values.
Results may differ from a plain program's by a relative error of at most 0.011.
Values may be sent and summed in bfloat16 or wider, within the bound.
A program may use at most 128 MiB of HBM per device.

v0:
```python
import jax
import jax.numpy as jnp
from jax import lax
from jax.sharding import PartitionSpec as P

FF = 7168
STEPS = 2


eps = 1e-05
learn_rate = 0.5


def partner(block, axis, apart):
    count = lax.axis_size(axis)
    route = []
    for low in range(count):
        high = low | 1 << apart
        if high != low and high < count:
            route += [(low, high), (high, low)]
    return lax.ppermute(block, axis, route)


def contract_rows(left, right):
    return lax.dot_general(
        left, right, (((0,), (0,)), ((), ())), preferred_element_type=jnp.float32
    )


def norm_backward(outputs, target_rows, norm_gain):
    squares = jnp.mean(outputs * outputs, axis=-1, keepdims=True)
    inverse = lax.rsqrt(squares + eps)
    normed = outputs * inverse
    weighted = (normed * norm_gain - target_rows.astype(jnp.float32)) * norm_gain
    cross_mean = jnp.mean(weighted * normed, axis=-1, keepdims=True)
    return (inverse * (weighted - normed * cross_mean)).astype(jnp.bfloat16)


def on_device(weights, hidden, targets, norm_gain, stragglers):
    replica_index = lax.axis_index("replica")
    levels = lax.axis_size("replica").bit_length() - 1
    factor = FF ** (-0.5)
    weight_block = weights[0]
    for update_step in range(STEPS):
        bit_index = update_step % levels
        hidden_rows = hidden[0, update_step]
        target_rows = targets[0, update_step]
        terms = factor * jnp.dot(hidden_rows, weight_block, preferred_element_type=jnp.float32)
        outputs = lax.psum(terms.astype(jnp.bfloat16), "tensor").astype(jnp.float32)
        grad_out = norm_backward(outputs, target_rows, norm_gain)
        grad_weight = (factor * contract_rows(hidden_rows, grad_out)).astype(jnp.bfloat16)
        updated = (
            weight_block.astype(jnp.float32) - learn_rate * grad_weight.astype(jnp.float32)
        ).astype(jnp.bfloat16)
        paired = partner(updated, "replica", bit_index)
        partner_index = jnp.bitwise_xor(replica_index, jnp.int32(1 << bit_index))
        mask_row = stragglers[update_step]
        self_late = lax.dynamic_index_in_dim(mask_row, replica_index, keepdims=False)
        partner_late = lax.dynamic_index_in_dim(mask_row, partner_index, keepdims=False)
        keep_pair = (self_late == 0) & (partner_late == 0)
        averaged = ((updated.astype(jnp.float32) + paired.astype(jnp.float32)) * 0.5).astype(
            jnp.bfloat16
        )
        weight_block = jnp.where(keep_pair, averaged, updated)
    return weight_block[None]


def solution(mesh):
    placed = (
        P("replica", "tensor", None),
        P("replica", None, None, "tensor"),
        P("replica", None, None, None),
        P(),
        P(),
    )
    return jax.shard_map(
        on_device,
        mesh=mesh,
        in_specs=placed,
        out_specs=P("replica", "tensor", None),
        check_vma=False,
    )
```

profile of v0, /device:TPU:0, one launch (start us, length us, event | category | flops | bytes accessed | tf_op | source)
XLA Modules:
  0.0 447.4 jit_solution(11788081942022073294)
XLA Ops:
  6.5 0.0 all-reduce.3.cloned.1.call-start
  6.5 8.9 %multiply_convert_fusion.5 = bf16[512,2048]{1,0:T(8,128)(2,1)} fusion(bf16[1,1792,2048]{2,1,0:T(8,128)(2,1)} %param.5, bf16[1,2,512,1792]{3,2,1,0:T(8,128)(2,1)} %param.6), kind=kOutput, calls=%fused_computation.38 | convolution fusion | flops 3760193536 | bytes 11272192 | tf_op jit(solution)/shard_map/dot_general | solution.py:48
  15.5 0.0 all-reduce.3.cloned.1.call-update
  15.5 0.0 copy-start.6
  15.5 0.2 all-reduce.5.cloned.1.call-start
  15.7 10.0 %copy.6 = bf16[1,1792,2048]{1,2,0:T(8,128)(2,1)} copy(bf16[1,1792,2048]{2,1,0:T(8,128)(2,1)} %param.5) | data formatting | bytes 14680064 | tf_op args[0]
  25.8 78.7 %all-reduce.3.cloned.1.call-done = bf16[512,2048]{1,0:T(8,128)(2,1)} async-done(((bf16[512,2048]{1,0:T(8,128)(2,1)}), bf16[512,2048]{1,0:T(8,128)(2,1)}) %all-reduce.3.cloned.1.call-update) | async-done | bytes 2097168 | tf_op jit(solution)/shard_map/psum | solution.py:49
  104.5 2.2 fusion.19
  106.7 0.0 copy-done.6
  106.8 3.7 fusion.15
  110.4 0.0 copy-done
  110.4 0.0 copy-done.4
  110.4 0.0 copy-start.7
  110.5 9.9 %fusion.1 = bf16[1792,2048]{0,1:T(8,128)(2,1)} fusion(bf16[1,1792,2048]{1,2,0:T(8,128)(2,1)} %copy.6, bf16[512,2048]{1,0:T(8,128)(2,1)S(1)} %copy-done, f32[512]{0:T(512)S(1)} %broadcast_multiply_fusion.1, f32[2048]{0:T(1024)S(1)} %copy-done.6, f32[512]{0:T(512)S(1)} %add_rsqrt_fusion.1, bf16[1,2,512,2048]{3,2,1,0:T(8,128)(2,1)S(1)} %copy-done.4, ...), kind=kOutput, calls=%fused_computation.3 | convolution fusion | flops 3794272256 | bytes 20721664 | tf_op jit(solution)/shard_map/dot_general | solution.py:25
  120.4 0.0 collective-permute-start
  120.4 0.0 copy-done.7
  120.4 0.7 constant_dynamic-slice_fusion
  122.3 10.1 %collective-permute-done = bf16[1792,2048]{0,1:T(8,128)(2,1)} collective-permute-done((bf16[1792,2048]{0,1:T(8,128)(2,1)}, bf16[1792,2048]{0,1:T(8,128)(2,1)}, u32[]{:S(2)}, u32[]{:S(2)}) %collective-permute-start) | collective-permute-done | bytes 7340064 | tf_op jit(solution)/shard_map/ppermute | solution.py:21
  132.4 13.1 %fusion.29 = bf16[512,2048]{1,0:T(8,128)(2,1)} fusion(bf16[1,2,512,1792]{3,2,1,0:T(8,128)(2,1)} %param.6, bf16[1792,2048]{0,1:T(8,128)(2,1)} %fusion.1, bf16[1792,2048]{0,1:T(8,128)(2,1)} %collective-permute-done, pred[]{:T(512)} %bitcast.1), kind=kOutput, calls=%fused_computation.39 | convolution fusion | flops 3782213632 | bytes 18612736 | tf_op jit(solution)/shard_map/dot_general | solution.py:48
  145.5 0.0 all-reduce.5.cloned.1.call-update
  145.5 85.3 %all-reduce.5.cloned.1.call-done = bf16[512,2048]{1,0:T(8,128)(2,1)} async-done(((bf16[512,2048]{1,0:T(8,128)(2,1)}), bf16[512,2048]{1,0:T(8,128)(2,1)}) %all-reduce.5.cloned.1.call-update) | async-done | bytes 2097168 | tf_op jit(solution)/shard_map/psum | solution.py:49
  230.9 2.2 fusion.26
  233.1 3.7 fusion.22
  236.8 0.0 copy-done.1
  236.8 14.6 %fusion = bf16[1792,2048]{0,1:T(8,128)(2,1)S(1)} fusion(bf16[512,2048]{1,0:T(8,128)(2,1)S(1)} %copy-done.1, f32[512]{0:T(512)S(1)} %broadcast_multiply_fusion, f32[512]{0:T(512)S(1)} %add_rsqrt_fusion, f32[2048]{0:T(1024)S(1)} %copy-done.6, bf16[1,2,512,2048]{3,2,1,0:T(8,128)(2,1)S(1)} %copy-done.5, bf16[1,2,512,1792]{3,2,1,0:T(8,128)(2,1)} %param.6, ...), kind=kOutput, calls=%fused_computation.1 | convolution fusion | flops 3816292352 | bytes 28062208 | tf_op jit(solution)/shard_map/dot_general | solution.py:25
  251.4 0.0 copy-start.2
  251.4 3.0 copy-done.2
  254.5 1.5 collective-permute-start.1
  257.3 156.6 %collective-permute-done.1 = bf16[1792,2048]{0,1:T(8,128)(2,1)S(1)} collective-permute-done((bf16[1792,2048]{0,1:T(8,128)(2,1)S(1)}, bf16[1792,2048]{0,1:T(8,128)(2,1)S(1)}, u32[]{:S(2)}, u32[]{:S(2)}) %collective-permute-start.1) | collective-permute-done | bytes 7340064 | tf_op jit(solution)/shard_map/ppermute | solution.py:21
  413.9 3.0 copy-done.3
  416.8 13.3 %fusion.4 = bf16[1,1792,2048]{1,2,0:T(8,128)(2,1)} fusion(bf16[1792,2048]{0,1:T(8,128)(2,1)} %copy-done.2, bf16[1792,2048]{0,1:T(8,128)(2,1)} %copy-done.3, pred[]{:T(512)} %bitcast), kind=kLoop, calls=%fused_computation.10 | loop fusion | flops 22020096 | bytes 22020096 | tf_op jit(solution)/shard_map/broadcast_in_dim | solution.py:65
  430.2 10.4 %copy.8 = bf16[1,1792,2048]{2,1,0:T(8,128)(2,1)} copy(bf16[1,1792,2048]{1,2,0:T(8,128)(2,1)} %fusion.4) | data formatting | bytes 14680064 | tf_op jit(solution)/shard_map/broadcast_in_dim | solution.py:65
  (11 shorter events, 0.0 us)
Async XLA Ops:
  6.5 98.0 %all-reduce.3.cloned.1.call-start = ((), (), s32[]{:S(2)}) async-start(), calls=%async_computation | async-start | bytes 4194304 | tf_op jit(solution)/shard_map/psum | solution.py:49
  15.5 91.2 %copy-start.6 = (f32[2048]{0:T(1024)S(1)}, f32[2048]{0:T(1024)}, u32[]{:S(2)}) copy-start(f32[2048]{0:T(1024)} %param.8) | copy-start | bytes 24580
  15.5 215.4 %all-reduce.5.cloned.1.call-start = ((), (), s32[]{:S(2)}) async-start(), calls=%async_computation.1 | async-start | bytes 4194304 | tf_op jit(solution)/shard_map/psum | solution.py:49
  104.5 5.9 %copy-start = (bf16[512,2048]{1,0:T(8,128)(2,1)S(1)}, bf16[512,2048]{1,0:T(8,128)(2,1)}, u32[]{:S(2)}) copy-start(bf16[512,2048]{1,0:T(8,128)(2,1)} %all-reduce.3.cloned.1.call-done) | copy-start | bytes 6291460
  104.5 5.9 %copy-start.4 = (bf16[1,2,512,2048]{3,2,1,0:T(8,128)(2,1)S(1)}, bf16[1,2,512,2048]{3,2,1,0:T(8,128)(2,1)}, u32[]{:S(2)}) copy-start(bf16[1,2,512,2048]{3,2,1,0:T(8,128)(2,1)} %param.7) | copy-start | bytes 12582916
  110.4 9.9 %copy-start.7 = (s32[2,8]{1,0:T(2,128)S(1)}, s32[2,8]{1,0:T(2,128)}, u32[]{:S(2)}) copy-start(s32[2,8]{1,0:T(2,128)} %param.9) | copy-start | bytes 196
  120.4 12.0 %collective-permute-start = (bf16[1792,2048]{0,1:T(8,128)(2,1)}, bf16[1792,2048]{0,1:T(8,128)(2,1)}, u32[]{:S(2)}, u32[]{:S(2)}) collective-permute-start(bf16[1792,2048]{0,1:T(8,128)(2,1)} %fusion.1), channel_id=1, source_target_pairs={{0,4},{4,0},{8,12},{12,8},{16,20},{20,16},{24,28},{28,24},{1,5},{5... | collective-permute-start | bytes 22020104 | tf_op jit(solution)/shard_map/ppermute | solution.py:21
  230.9 5.9 %copy-start.1 = (bf16[512,2048]{1,0:T(8,128)(2,1)S(1)}, bf16[512,2048]{1,0:T(8,128)(2,1)}, u32[]{:S(2)}) copy-start(bf16[512,2048]{1,0:T(8,128)(2,1)} %all-reduce.5.cloned.1.call-done) | copy-start | bytes 6291460
  230.9 5.9 %copy-start.5 = (bf16[1,2,512,2048]{3,2,1,0:T(8,128)(2,1)S(1)}, bf16[1,2,512,2048]{3,2,1,0:T(8,128)(2,1)}, u32[]{:S(2)}) copy-start(bf16[1,2,512,2048]{3,2,1,0:T(8,128)(2,1)} %param.7) | copy-start | bytes 12582916
  251.4 3.1 copy-start.2
  254.5 159.4 %collective-permute-start.1 = (bf16[1792,2048]{0,1:T(8,128)(2,1)S(1)}, bf16[1792,2048]{0,1:T(8,128)(2,1)S(1)}, u32[]{:S(2)}, u32[]{:S(2)}) collective-permute-start(bf16[1792,2048]{0,1:T(8,128)(2,1)S(1)} %fusion), channel_id=1, source_target_pairs={{0,8},{8,0},{4,12},{12,4},{16,24},{24,16},{20,28},{28,20},{1,9},{9... | collective-permute-start | bytes 22020104 | tf_op jit(solution)/shard_map/ppermute | solution.py:21
  413.9 3.0 copy-start.3
Sparse Core Ops, SparseCore 0:
  15.6 88.8 all-reduce.2
  145.7 85.1 all-reduce.4
where the time goes:
time: 448 us; the launch traced here: 447 us
  waiting for transfers between devices  331 us (74%)
  matrix products  46.6 us (10%)
  local copies, waits for them, and re-layouts  27.2 us (6%)
  other arithmetic  25.2 us (6%)
  between operations  16 us (4%)
    ppermute x2, waiting for transfers between devices, partner(): return lax.ppermute(block, axis, route)  167 us
    psum x2, waiting for transfers between devices, on_device(): outputs = lax.psum(terms.astype(jnp.bfloat16), 'tensor').astype(jnp.float32)  164 us
    dot_general x2, matrix products, contract_rows(): lax.dot_general(left, right, (((0,), (0,)), ((), ())), preferred_element_...  24.5 us
    dot_general x2, matrix products, on_device(): jnp.dot(hidden_rows, weight_block, preferred_element_type=jnp.float32)  22.1 us
    unnamed x17, local copies, waits for them, and re-layouts  16.1 us
    broadcast_in_dim x1, other arithmetic, on_device(): return weight_block[None]  13.3 us
    broadcast_in_dim x1, local copies, waits for them, and re-layouts, on_device(): return weight_block[None]  10.4 us
  transfers between devices with their start and end apart: 4, of which 4 were waited for; matrix products, arithmetic and copies ran while one was open for 2% of the time, Pallas kernels for 0%

commit v1 on v0

v1 whole, which is shorter than its diff:
```python
import functools

import jax
import jax.numpy as jnp
from jax import lax
from jax.experimental import pallas as pl
from jax.experimental.pallas import tpu as pltpu
from jax.sharding import PartitionSpec as P

FF = 7168
STEPS = 2


eps = 1e-05
learn_rate = 0.5

MESH = pl.DeviceIdType.MESH
TILE = 256
ROWS = 256
PIECES = 16
AHEAD = 2
BESIDE = 6


def partner(block, axis, apart):
    count = lax.axis_size(axis)
    route = []
    for low in range(count):
        high = low | 1 << apart
        if high != low and high < count:
            route += [(low, high), (high, low)]
    return lax.ppermute(block, axis, route)


def contract_rows(left, right):
    return lax.dot_general(
        left, right, (((0,), (0,)), ((), ())), preferred_element_type=jnp.float32
    )


def norm_backward(outputs, target_rows, norm_gain):
    squares = jnp.mean(outputs * outputs, axis=-1, keepdims=True)
    inverse = lax.rsqrt(squares + eps)
    normed = outputs * inverse
    weighted = (normed * norm_gain - target_rows.astype(jnp.float32)) * norm_gain
    cross_mean = jnp.mean(weighted * normed, axis=-1, keepdims=True)
    return (inverse * (weighted - normed * cross_mean)).astype(jnp.bfloat16)


def descend(weight_block, hidden_rows, grad_out):
    factor = FF ** (-0.5)
    grad_weight = (factor * contract_rows(hidden_rows, grad_out)).astype(jnp.bfloat16)
    return (
        weight_block.astype(jnp.float32) - learn_rate * grad_weight.astype(jnp.float32)
    ).astype(jnp.bfloat16)


def step_kernel(apart, last, *refs):
    hidden_ref, weight_ref, target_ref, gain_ref, cargo_ref = refs[:5]
    if last:
        grad_ref, landed_ref, paired_ref = refs[5:8]
        rest = refs[8:]
    else:
        grad_ref, landed_ref = refs[5:7]
        rest = refs[7:]
    terms, in_right, in_left, out_right, out_left = rest[:5]
    right_send, right_recv, left_send, left_recv, cargo_send, cargo_recv = rest[5:11]
    if last:
        far_grad, grad_send, grad_recv, share_send, share_recv = rest[11:]

    count = lax.axis_size("tensor")
    me = lax.axis_index("tensor")
    replica = lax.axis_index("replica")
    step = 1 << apart
    far = replica + step - 2 * step * ((replica // step) % 2)
    last_rank = count - 1
    factor = FF ** (-0.5)

    barrier = pltpu.get_barrier_semaphore()
    pl.semaphore_signal(barrier, inc=1, device_id=(far, me), device_id_type=MESH)
    for hop in range(1, count):
        peer = lax.rem(me + hop, count)
        pl.semaphore_signal(barrier, inc=1, device_id=(replica, peer), device_id_type=MESH)
    pl.semaphore_wait(barrier, count)

    depth = cargo_ref.shape[0] // PIECES

    def cargo(index):
        span = pl.ds(index * depth, depth)
        return pltpu.make_async_remote_copy(
            src_ref=cargo_ref.at[span], dst_ref=landed_ref.at[span],
            send_sem=cargo_send.at[index], recv_sem=cargo_recv.at[index],
            device_id=(far, me), device_id_type=MESH,
        )

    for index in range(AHEAD):
        cargo(index).start()

    @pl.when(me == 0)
    def _():
        in_right[...] = jnp.zeros_like(in_right)

    @pl.when(me == last_rank)
    def _():
        in_left[...] = jnp.zeros_like(in_left)

    tiles, tokens = terms.shape[0], terms.shape[1]
    halves = tokens // ROWS
    chunks = tiles * halves

    def place(chunk):
        return chunk // halves, pl.ds(pl.multiple_of((chunk % halves) * ROWS, ROWS), ROWS)

    def right_copy(chunk):
        tile, rows = place(chunk)
        return pltpu.make_async_remote_copy(
            src_ref=out_right.at[tile, rows], dst_ref=in_right.at[tile, rows],
            send_sem=right_send.at[chunk], recv_sem=right_recv.at[chunk],
            device_id=(replica, lax.rem(me + 1, count)), device_id_type=MESH,
        )

    def left_copy(chunk):
        tile, rows = place(chunk)
        return pltpu.make_async_remote_copy(
            src_ref=out_left.at[tile, rows], dst_ref=in_left.at[tile, rows],
            send_sem=left_send.at[chunk], recv_sem=left_recv.at[chunk],
            device_id=(replica, lax.rem(me + count - 1, count)), device_id_type=MESH,
        )

    def turn(now, _):
        @pl.when(now < chunks)
        def _():
            tile, rows = place(now)
            columns = pl.ds(pl.multiple_of(tile * TILE, TILE), TILE)
            terms[tile, rows, :] = factor * jnp.dot(
                hidden_ref[rows, :], weight_ref[:, columns], preferred_element_type=jnp.float32
            )

        rightward = now - me

        @pl.when((rightward >= 0) & (rightward < chunks))
        def _():
            @pl.when(me > 0)
            def _():
                right_copy(rightward).wait_recv()

            @pl.when(me < last_rank)
            def _():
                tile, rows = place(rightward)
                total = terms[tile, rows, :] + in_right[tile, rows, :].astype(jnp.float32)
                out_right[tile, rows, :] = total.astype(jnp.bfloat16)
                right_copy(rightward).start()

        leftward = now - (last_rank - me)

        @pl.when((leftward >= 0) & (leftward < chunks))
        def _():
            @pl.when(me < last_rank)
            def _():
                left_copy(leftward).wait_recv()

            @pl.when(me > 0)
            def _():
                tile, rows = place(leftward)
                total = terms[tile, rows, :] + in_left[tile, rows, :].astype(jnp.float32)
                out_left[tile, rows, :] = total.astype(jnp.bfloat16)
                left_copy(leftward).start()

        if last:
            pace = (chunks + last_rank) // (BESIDE - AHEAD)
            index = AHEAD + now // pace

            @pl.when((now % pace == pace - 1) & (index < BESIDE))
            def _():
                cargo(index).start()

        return 0

    if not last:
        for index in range(AHEAD, PIECES):
            cargo(index).start()
    lax.fori_loop(0, chunks + last_rank, turn, 0)

    block = 32

    def normalise(index, _):
        rows = pl.ds(pl.multiple_of(index * block, block), block)
        outputs = jnp.concatenate(
            [
                terms[tile, rows, :]
                + in_right[tile, rows, :].astype(jnp.float32)
                + in_left[tile, rows, :].astype(jnp.float32)
                for tile in range(tiles)
            ],
            axis=1,
        )
        grad_ref[rows, :] = norm_backward(outputs, target_ref[rows, :], gain_ref[...])
        return 0

    lax.fori_loop(0, tokens // block, normalise, 0)

    if last:
        part = tokens // count
        mine = pl.ds(pl.multiple_of(me * part, part), part)
        across = pltpu.make_async_remote_copy(
            src_ref=grad_ref.at[mine], dst_ref=far_grad.at[mine],
            send_sem=grad_send, recv_sem=grad_recv,
            device_id=(far, me), device_id_type=MESH,
        )
        across.start()
        for index in range(BESIDE, PIECES):
            cargo(index).start()
        across.wait_recv()

        def share(hop):
            return pltpu.make_async_remote_copy(
                src_ref=far_grad.at[mine], dst_ref=far_grad.at[mine],
                send_sem=share_send.at[hop - 1], recv_sem=share_recv.at[hop - 1],
                device_id=(replica, lax.rem(me + hop, count)), device_id_type=MESH,
            )

        for hop in range(1, count):
            share(hop).start()
        for hop in range(1, count):
            share(hop).wait_recv()
        paired_ref[...] = far_grad[...]
        for hop in range(1, count):
            share(hop).wait_send()
        across.wait_send()

    def drain(chunk, _):
        @pl.when(me < last_rank)
        def _():
            right_copy(chunk).wait_send()

        @pl.when(me > 0)
        def _():
            left_copy(chunk).wait_send()

        return 0

    lax.fori_loop(0, chunks, drain, 0)
    for index in range(PIECES):
        cargo(index).wait()


def run_step(hidden_rows, weight_block, target_rows, norm_gain, cargo, apart, last):
    tokens, features = target_rows.shape
    tiles = features // TILE
    chunks = tiles * (tokens // ROWS)
    count = lax.axis_size("tensor")
    vmem = pl.BlockSpec(memory_space=pltpu.VMEM)
    anywhere = pl.BlockSpec(memory_space=pl.ANY)
    gradient = jax.ShapeDtypeStruct((tokens, features), jnp.bfloat16)
    landed = jax.ShapeDtypeStruct(cargo.shape, cargo.dtype)
    travelling = pltpu.VMEM((tiles, tokens, TILE), jnp.bfloat16)
    scratch = [pltpu.VMEM((tiles, tokens, TILE), jnp.float32)] + [travelling] * 4
    scratch += [pltpu.SemaphoreType.DMA((chunks,))] * 4 + [pltpu.SemaphoreType.DMA((PIECES,))] * 2
    if last:
        scratch += [pltpu.VMEM((tokens, features), jnp.bfloat16)]
        scratch += [pltpu.SemaphoreType.DMA] * 2 + [pltpu.SemaphoreType.DMA((count - 1,))] * 2
    return pl.pallas_call(
        functools.partial(step_kernel, apart, last),
        out_shape=(gradient, landed) + ((gradient,) if last else ()),
        in_specs=[vmem] * 4 + [anywhere],
        out_specs=(vmem, anywhere) + ((vmem,) if last else ()),
        scratch_shapes=scratch,
        compiler_params=pltpu.CompilerParams(
            collective_id=int(last), has_side_effects=True, vmem_limit_bytes=56 << 20
        ),
    )(hidden_rows, weight_block, target_rows, norm_gain[None], cargo)


def on_device(weights, hidden, targets, norm_gain, stragglers):
    replica_index = lax.axis_index("replica")
    weight_block = weights[0]

    def mixed(updated, paired, update_step):
        partner_index = jnp.bitwise_xor(replica_index, jnp.int32(1 << update_step))
        mask_row = stragglers[update_step]
        self_late = lax.dynamic_index_in_dim(mask_row, replica_index, keepdims=False)
        partner_late = lax.dynamic_index_in_dim(mask_row, partner_index, keepdims=False)
        keep_pair = (self_late == 0) & (partner_late == 0)
        averaged = ((updated.astype(jnp.float32) + paired.astype(jnp.float32)) * 0.5).astype(
            jnp.bfloat16
        )
        return jnp.where(keep_pair, averaged, updated)

    first, second = hidden[0, 0], hidden[0, 1]
    grad_out, paired_hidden = run_step(
        first, weight_block, targets[0, 0], norm_gain, second, 1, False
    )
    updated = descend(weight_block, first, grad_out)
    weight_block = mixed(updated, partner(updated, "replica", 0), 0)
    grad_out, paired_weight, paired_grad = run_step(
        second, weight_block, targets[0, 1], norm_gain, weight_block, 1, True
    )
    updated = descend(weight_block, second, grad_out)
    paired = descend(paired_weight, paired_hidden, paired_grad)
    return mixed(updated, paired, 1)[None]


def solution(mesh):
    placed = (
        P("replica", "tensor", None),
        P("replica", None, None, "tensor"),
        P("replica", None, None, None),
        P(),
        P(),
    )
    return jax.shard_map(
        on_device,
        mesh=mesh,
        in_specs=placed,
        out_specs=P("replica", "tensor", None),
        check_vma=False,
    )
```

time: 448 us -> 351 us (0.78)
  waiting for transfers between devices: 331 us -> 8.95 us
  Pallas kernels: 0 us -> 284 us
  local copies, waits for them, and re-layouts: 27.2 us -> 7.67 us
  matrix products: 46.6 us -> 31.6 us
  between operations: 16 us -> 2.47 us
  other arithmetic: 25.2 us -> 16.8 us
    pallas_call x0 -> x2, Pallas kernels: none -> 284 us  [run_step(): pl.pallas_call(functools.partial(step_kernel, apart, last), out_shape=(gr...]
    psum x2 -> x0, waiting for transfers between devices: 164 us -> none  [on_device(): outputs = lax.psum(terms.astype(jnp.bfloat16), 'tensor').astype(jnp.float32)]
    ppermute x2 -> x1, waiting for transfers between devices: 167 us -> 8.95 us  [partner(): return lax.ppermute(block, axis, route)]
    dot_general x2 -> x0, matrix products: 22.1 us -> none  [on_device(): jnp.dot(hidden_rows, weight_block, preferred_element_type=jnp.float32)]
    select_n x0 -> x1, other arithmetic: none -> 16.8 us  [mixed(): return jnp.where(keep_pair, averaged, updated)]
    unnamed x17 -> x16, local copies, waits for them, and re-layouts: 16.1 us -> 0.04 us
    broadcast_in_dim x1 -> x0, other arithmetic: 13.3 us -> none  [on_device(): return weight_block[None]]
    reduce_sum x4 -> x0, other arithmetic: 11.8 us -> none  [the longest x2 7.35 us: norm_backward(): cross_mean = jnp.mean(weighted * normed, axis=-1, keepdims=True)]
  transfers between devices with their start and end apart: 4 -> 1, of which waited for: 4 -> 1; matrix products, arithmetic and copies ran while one was open for 2% -> 0% of each run, Pallas kernels for 0% -> 0%
where the time goes in v1:
time: 351 us
  Pallas kernels  284 us (81%)
  matrix products  31.6 us (9%)
  other arithmetic  16.8 us (5%)
  waiting for transfers between devices  8.95 us (3%)
  local copies, waits for them, and re-layouts  7.67 us (2%)
    pallas_call x2, Pallas kernels, run_step(): pl.pallas_call(functools.partial(step_kernel, apart, last), out_shape=(gr...  284 us
    dot_general x3, matrix products, contract_rows(): lax.dot_general(left, right, (((0,), (0,)), ((), ())), preferred_element_...  31.6 us
    select_n x1, other arithmetic, mixed(): return jnp.where(keep_pair, averaged, updated)  16.8 us
    ppermute x1, waiting for transfers between devices, partner(): return lax.ppermute(block, axis, route)  8.95 us
  transfers between devices with their start and end apart: 1, of which 1 were waited for; matrix products, arithmetic and copies ran while one was open for 0% of the time, Pallas kernels for 0%

profile of v1, /device:TPU:0, one launch (start us, length us, event | category | flops | bytes accessed | tf_op | source)
XLA Modules:
  0.0 351.1 jit_solution(3320863035040845888)
XLA Ops:
  0.0 0.0 copy-start
  0.0 4.3 %slice_bitcast_fusion.3 = (bf16[512,1792]{1,0:T(8,128)(2,1)}, bf16[512,1792]{1,0:T(8,128)(2,1)}) fusion(bf16[1,2,512,1792]{3,2,1,0:T(8,128)(2,1)} %param.6), kind=kLoop, calls=%fused_computation.16 | loop fusion | bytes 7340032 | tf_op jit(solution)/shard_map/squeeze | solution.py:289
  4.3 0.0 copy-done
  4.3 0.0 slice-start.2
  4.3 2.7 slice_bitcast_fusion
  7.0 0.0 slice-start.3
  7.0 92.3 %shard_map.55 = (bf16[512,2048]{1,0:T(8,128)(2,1)}, bf16[512,1792]{1,0:T(8,128)(2,1)}) custom-call(bf16[512,1792]{1,0:T(8,128)(2,1)} %get-tuple-element.17.refs_0_, bf16[1792,2048]{1,0:T(8,128)(2,1)} %bitcast.33, bf16[512,2048]{1,0:T(8,128)(2,1)} %get-tuple-element.16.refs_2_, f32[1,2048]{1,0:T(1,128)} %bitcast.36, ...), custom_call_target="tpu_custom_call" | custom-call | tf_op jit(solution)/shard_map/pallas_call | solution.py:262
  99.3 0.0 slice-done.2
  99.3 0.0 slice-done.3
  99.3 0.0 copy-start.2
  99.4 10.1 %fusion.1 = bf16[1792,2048]{1,0:T(8,128)(2,1)} fusion(bf16[512,2048]{1,0:T(8,128)(2,1)} %get-tuple-element.10, bf16[1,1792,2048]{2,1,0:T(8,128)(2,1)S(1)} %bitcast.35, bf16[1,2,512,1792]{3,2,1,0:T(8,128)(2,1)} %param.6), kind=kOutput, calls=%fused_computation.3 | convolution fusion | flops 3783786496 | bytes 18612224 | tf_op jit(solution)/shard_map/dot_general | solution.py:36
  109.4 0.0 collective-permute-start
  109.4 0.0 copy-done.2
  109.4 0.7 constant_dynamic-slice_fusion
  112.5 8.9 %collective-permute-done = bf16[1792,2048]{1,0:T(8,128)(2,1)} collective-permute-done((bf16[1792,2048]{1,0:T(8,128)(2,1)}, bf16[1792,2048]{1,0:T(8,128)(2,1)}, u32[]{:S(2)}, u32[]{:S(2)}) %collective-permute-start) | collective-permute-done | bytes 7340064 | tf_op jit(solution)/shard_map/ppermute | solution.py:32
  121.4 16.8 %fusion.2.refs_1_.refs_4_ = bf16[1792,2048]{1,0:T(8,128)(2,1)} fusion(bf16[1792,2048]{1,0:T(8,128)(2,1)} %fusion.1, bf16[1792,2048]{1,0:T(8,128)(2,1)} %collective-permute-done, pred[]{:T(512)} %bitcast.1), kind=kLoop, calls=%fused_computation.10 | loop fusion | flops 22020096 | bytes 22020096 | tf_op jit(solution)/shard_map/jit(_where)/select_n | solution.py:287
  138.2 0.0 copy-start.1
  138.2 0.0 slice-start
  138.2 191.3 %shard_map.56 = (bf16[512,2048]{1,0:T(8,128)(2,1)}, bf16[1792,2048]{1,0:T(8,128)(2,1)}, bf16[512,2048]{1,0:T(8,128)(2,1)}) custom-call(bf16[512,1792]{1,0:T(8,128)(2,1)} %get-tuple-element.18.refs_4_.refs_0_, bf16[1792,2048]{1,0:T(8,128)(2,1)} %fusion.2.refs_1_.refs_4_, bf16[512,2048]{1,0:T(8,128)(2,1)} %get-tuple-element.15.refs_2_, f32[1,2048]{1,0:T(1,128)} %bitcast.37, ...), custom_call_target="tpu_custom_call" | custom-call | tf_op jit(solution)/shard_map/pallas_call | solution.py:262
  329.5 0.0 copy-done.1
  329.5 0.0 slice-start.1
  329.5 0.0 copy-start.3
  329.5 7.9 %multiply_convert_fusion.2 = bf16[2048,1792]{0,1:T(8,128)(2,1)} fusion(bf16[512,2048]{1,0:T(8,128)(2,1)} %get-tuple-element.11, bf16[1,2,512,1792]{3,2,1,0:T(8,128)(2,1)S(1)} %copy-done.1), kind=kOutput, calls=%fused_computation.7 | convolution fusion | flops 3765436416 | bytes 11272192 | tf_op jit(solution)/shard_map/dot_general | solution.py:36
  337.5 0.0 slice-done
  337.5 0.0 slice-done.1
  337.5 0.0 copy-done.3
  337.5 13.6 %fusion.4 = bf16[1,1792,2048]{2,1,0:T(8,128)(2,1)} fusion(bf16[1792,2048]{1,0:T(8,128)(2,1)} %get-tuple-element.12, bf16[2048,1792]{0,1:T(8,128)(2,1)} %multiply_convert_fusion.2, bf16[1792,2048]{1,0:T(8,128)(2,1)S(1)} %bitcast.32, pred[]{:T(512)} %bitcast, bf16[512,1792]{1,0:T(8,128)(2,1)} %get-tuple-element.13, bf16[512,2048]{1,0:T(8,128)(2,1)S(1)} %copy-done.3), kind=kOutput, calls=%fused_computation.12 | convolution fusion | flops 3824156672 | bytes 33292288 | tf_op jit(solution)/shard_map/dot_general | solution.py:36
  (3 shorter events, 0.0 us)
Async XLA Ops:
  0.0 4.3 %copy-start = (bf16[1,2,512,2048]{3,2,1,0:T(8,128)(2,1)S(1)}, bf16[1,2,512,2048]{3,2,1,0:T(8,128)(2,1)}, u32[]{:S(2)}) copy-start(bf16[1,2,512,2048]{3,2,1,0:T(8,128)(2,1)} %param.7) | copy-start | bytes 12582916
  4.3 95.0 %slice-start.2 = ((s8[7340032]{0:T(1024)(128)(4,1)}), s8[4194304]{0:T(1024)(128)(4,1)S(1)}, s32[]{:S(2)}) async-start(s8[7340032]{0:T(1024)(128)(4,1)} %bitcast.34), calls=%async_computation.2 | async-start | bytes 8388608
  7.0 92.4 %slice-start.3 = ((s8[7340032]{0:T(1024)(128)(4,1)}), s8[3145728]{0:T(1024)(128)(4,1)S(1)}, s32[]{:S(2)}) async-start(s8[7340032]{0:T(1024)(128)(4,1)} %bitcast.34), calls=%async_computation.3 | async-start | bytes 6291456
  99.3 10.1 %copy-start.2 = (s32[2,8]{1,0:T(2,128)S(1)}, s32[2,8]{1,0:T(2,128)}, u32[]{:S(2)}) copy-start(s32[2,8]{1,0:T(2,128)} %param.9) | copy-start | bytes 196
  109.4 12.0 %collective-permute-start = (bf16[1792,2048]{1,0:T(8,128)(2,1)}, bf16[1792,2048]{1,0:T(8,128)(2,1)}, u32[]{:S(2)}, u32[]{:S(2)}) collective-permute-start(bf16[1792,2048]{1,0:T(8,128)(2,1)} %fusion.1), channel_id=1, source_target_pairs={{0,4},{4,0},{8,12},{12,8},{16,20},{20,16},{24,28},{28,24},{1,5},{5... | collective-permute-start | bytes 22020104 | tf_op jit(solution)/shard_map/ppermute | solution.py:32
  138.2 191.3 %copy-start.1 = (bf16[1,2,512,1792]{3,2,1,0:T(8,128)(2,1)S(1)}, bf16[1,2,512,1792]{3,2,1,0:T(8,128)(2,1)}, u32[]{:S(2)}) copy-start(bf16[1,2,512,1792]{3,2,1,0:T(8,128)(2,1)} %param.6) | copy-start | bytes 11010052
  138.2 199.2 %slice-start = ((s8[7340032]{0:T(1024)(128)(4,1)}), s8[3145728]{0:T(1024)(128)(4,1)S(1)}, s32[]{:S(2)}) async-start(s8[7340032]{0:T(1024)(128)(4,1)} %bitcast.31), calls=%async_computation | async-start | bytes 6291456
  329.5 8.0 %slice-start.1 = ((s8[7340032]{0:T(1024)(128)(4,1)}), s8[4194304]{0:T(1024)(128)(4,1)S(1)}, s32[]{:S(2)}) async-start(s8[7340032]{0:T(1024)(128)(4,1)} %bitcast.31), calls=%async_computation.1 | async-start | bytes 8388608
  329.5 8.0 %copy-start.3 = (bf16[512,2048]{1,0:T(8,128)(2,1)S(1)}, bf16[512,2048]{1,0:T(8,128)(2,1)}, u32[]{:S(2)}) copy-start(bf16[512,2048]{1,0:T(8,128)(2,1)} %get-tuple-element.14) | copy-start | bytes 6291460
